TPU v7x, 32 devices: a whole 2x2x4 slice. The times are simulated.
32 devices in a mesh: seq: 8 (over z, x), head: 4 (over y, core).
Axes of the slice: x: 2, y: 2, z: 4, core: 2. Of those that a mesh axis runs over, the one named last changes fastest.
Arguments:
- queries: bfloat16 [2048, 64, 128], P('seq', 'head'), may hold values from -360 to 360
- head_weights: bfloat16 [2048, 64], P('seq', 'head'), may hold values from -0.75 to 0.75
- keys: bfloat16 [2048, 128], P('seq'), may hold values from -6 to 6
- targets: bfloat16 [2048, 2048], P('seq'), may hold values from 0.0099487305 to 10
- chosen: int32 [16, 16], P('seq'), may hold values from -1 to 15, as said below
- tile_block: int32 [16], replicated, may hold values from 0 to 15, as said below
Outputs:
- query_grads: bfloat16 [2048, 64, 128], P('seq', 'head')
- weight_grads: float32 [2048, 64], P('seq', 'head')
- key_grads: float32 [2048, 128], P('seq')
- loss: float32 [], replicated
Inputs may be any that keep to these rules, and one draw needn't show every extreme that they name: `tile_block`: a permutation of 0 to 15; each aligned group of 4 stored positions holds the global blocks of that same group. `chosen`: slot 0 of stored tile p is tile_block[p]; live entries of a row are distinct, none exceeds tile_block[p], and they precede the -1 entries; over all tiles of one device of seq, at most 1 distinct live block is stored on any one other device.
All inputs are finite; a program needn't handle non-finite values.
Results may differ from a plain program's by a relative error of at most 0.0095.
Values may be sent and summed in bfloat16 or wider, within the bound.
No kernel may reach another device: no remote copies, remote signals or barrier semaphores. Data moves between devices by JAX's collectives and lax.ppermute only.
A program may use at most 128 MiB of HBM per device.

v0:
```python
import jax
import jax.numpy as jnp
from jax import lax
from jax.sharding import PartitionSpec as P

BLOCK = 128
SLOTS = 16
CAP = 1
KEYS = 2048
loss_scale = 4194304.0


def row_statistics(score_part, mask_part, target_part):
    row_max = jnp.max(jnp.where(mask_part, score_part, -1e30), axis=1)
    exp_terms = jnp.where(
        mask_part, jnp.exp(jnp.where(mask_part, score_part - row_max[:, None], 0.0)), 0.0
    )
    return (row_max, jnp.sum(exp_terms, axis=1), jnp.sum(target_part, axis=1))


def local(queries, head_weights, keys, targets, chosen, tile_block):
    row_count, heads_here, key_width = queries.shape
    tiles_here = row_count // BLOCK
    block_count = tile_block.shape[0]
    owner_count = block_count // tiles_here
    score_scale = key_width ** (-0.5)
    seq_index = lax.axis_index("seq")
    head_index = lax.axis_index("head")
    is_first = (head_index == 0).astype(jnp.float32)
    positions = jnp.arange(block_count, dtype=jnp.int32)
    home_of = jnp.sum(
        jnp.where(tile_block[None, :] == positions[:, None], positions[None, :], 0), axis=1
    )
    live_slot = chosen >= 0
    position = home_of[jnp.maximum(chosen, 0)]
    owner_index = position // tiles_here
    local_slot = position % tiles_here
    own_block = lax.dynamic_slice_in_dim(tile_block, seq_index * tiles_here, tiles_here)
    offsets = jnp.arange(BLOCK, dtype=jnp.int32)
    causal = offsets[None, :] <= offsets[:, None]
    own_slot = chosen == own_block[:, None]
    live_mask = live_slot[:, None, :, None] & (
        (~own_slot)[:, None, :, None] | causal[None, :, None, :]
    )
    live_mask = live_mask.reshape(row_count, KEYS)
    key_blocks = keys.reshape(tiles_here, BLOCK, key_width)
    remote = live_slot & (owner_index != seq_index)
    remote_pos = jnp.where(remote, position, -1).reshape(-1)
    wanted = jnp.any(remote_pos[:, None] == positions[None, :], axis=0).reshape(
        owner_count, tiles_here
    )
    slot_rank = jnp.cumsum(wanted.astype(jnp.int32), axis=1) - 1
    local_iota = jnp.arange(tiles_here, dtype=jnp.int32)
    request = jnp.stack(
        [jnp.sum(jnp.where(wanted & (slot_rank == 0), local_iota[None, :], 0), axis=1)], axis=1
    )
    asked_slots = lax.all_to_all(request, "seq", split_axis=0, concat_axis=0, tiled=True)
    reply_blocks = key_blocks[asked_slots]
    arrived = lax.all_to_all(reply_blocks, "seq", split_axis=0, concat_axis=0, tiled=True)
    key_table = jnp.concatenate(
        [key_blocks, arrived.reshape(owner_count * CAP, BLOCK, key_width)], axis=0
    )
    table_index = jnp.where(
        owner_index == seq_index,
        local_slot,
        tiles_here + owner_index * CAP + slot_rank[owner_index, local_slot],
    )
    table_index = jnp.where(live_slot, table_index, 0)
    fetched = key_table[table_index]
    query_tiles = queries.reshape(tiles_here, BLOCK, heads_here, key_width)
    weight_tiles = head_weights.astype(jnp.float32).reshape(tiles_here, BLOCK, heads_here)

    def dot_values(query_tile, key_tile):
        return jnp.einsum(
            "qhd,kd->qhk",
            query_tile,
            key_tile.reshape(-1, key_width),
            preferred_element_type=jnp.float32,
        )

    def forward(operands):
        query_tile, weight_tile, key_tile = operands
        values = dot_values(query_tile, key_tile)
        return score_scale * jnp.sum(jnp.maximum(values, 0.0) * weight_tile[:, :, None], axis=1)

    partial_value = lax.map(forward, (query_tiles, weight_tiles, fetched)).reshape(row_count, KEYS)
    target_vals = jnp.where(live_mask, targets.astype(jnp.float32), 0.0)
    pair_local = jnp.sum(live_mask.astype(jnp.float32))
    score_part = lax.psum(partial_value, "head")
    row_max, row_norm, row_target = row_statistics(score_part, live_mask, target_vals)
    target_prob = jnp.where(live_mask, target_vals / row_target[:, None], 0.0)
    kl_cols = jnp.sum(
        jnp.where(
            live_mask,
            target_prob * (jnp.log(jnp.where(live_mask, target_prob, 1.0)) - score_part),
            0.0,
        )
    )
    lse_sum = jnp.sum(row_max + jnp.log(row_norm))
    loss_part = is_first * (kl_cols + lse_sum)
    loss_total, pair_count = lax.psum((loss_part, is_first * pair_local), ("seq", "head"))
    softmax_vals = (
        jnp.where(live_mask, jnp.exp(jnp.where(live_mask, score_part - row_max[:, None], 0.0)), 0.0)
        / row_norm[:, None]
    )
    grad_part = loss_scale * KEYS * (softmax_vals - target_prob) / pair_count
    grad_tiles = grad_part.reshape(tiles_here, BLOCK, KEYS)

    def backward(operands):
        query_tile, weight_tile, key_tile, grad_tile = operands
        key_rows = key_tile.reshape(-1, key_width)
        values = dot_values(query_tile, key_tile)
        weight_grad = score_scale * jnp.sum(
            jnp.maximum(values, 0.0) * grad_tile[:, None, :], axis=2
        )
        dot_grads = (
            score_scale
            * weight_tile[:, :, None]
            * grad_tile[:, None, :]
            * (values > 0).astype(jnp.float32)
        ).astype(jnp.bfloat16)
        query_grad = jnp.einsum(
            "qhk,kd->qhd", dot_grads, key_rows, preferred_element_type=jnp.float32
        ).astype(jnp.bfloat16)
        key_grad = jnp.einsum(
            "qhk,qhd->kd", dot_grads, query_tile, preferred_element_type=jnp.float32
        )
        return (query_grad, weight_grad, key_grad.reshape(SLOTS, BLOCK, key_width))

    query_grads, weight_grads, key_parts = lax.map(
        backward, (query_tiles, weight_tiles, fetched, grad_tiles)
    )
    slot_grads = key_parts.reshape(tiles_here * SLOTS, BLOCK, key_width)
    spread = jax.ops.segment_sum(
        slot_grads, table_index.reshape(-1), num_segments=tiles_here + owner_count * CAP
    )
    returned = lax.all_to_all(
        spread[tiles_here:].reshape(owner_count, CAP, BLOCK, key_width).astype(jnp.bfloat16),
        "seq",
        split_axis=0,
        concat_axis=0,
        tiled=True,
    ).astype(jnp.float32)
    owned_grad = spread[:tiles_here] + jax.ops.segment_sum(
        returned.reshape(owner_count * CAP, BLOCK, key_width),
        asked_slots.reshape(-1),
        num_segments=tiles_here,
    )
    key_grads = lax.psum(owned_grad.astype(jnp.bfloat16), "head").astype(jnp.float32)
    return (
        query_grads.reshape(row_count, heads_here, key_width),
        weight_grads.reshape(row_count, heads_here),
        key_grads.reshape(row_count, key_width),
        KEYS * loss_total / pair_count,
    )


def solution(mesh):
    placed = (
        P("seq", "head", None),
        P("seq", "head"),
        P("seq", None),
        P("seq", None),
        P("seq", None),
        P(),
    )
    return jax.shard_map(
        local,
        mesh=mesh,
        in_specs=placed,
        out_specs=(P("seq", "head", None), P("seq", "head"), P("seq", None), P()),
        check_vma=False,
    )
```

profile of v0, /device:TPU:0, one launch (start us, length us, event | category | flops | bytes accessed | tf_op | source)
XLA Modules:
  0.0 263.6 jit_solution(3088929878997966264)
XLA Ops:
  11.5 7.3 %all-to-all-start = ((s32[8,1,1]{2,1,0:T(1,128)}), s32[8,1,1]{2,1,0:T(1,128)S(1)}, u32[]{:S(2)}, u32[]{:S(2)}) async-start(s32[8,1,1]{2,1,0:T(1,128)} %copy.39), calls=%async_computation | async-start | bytes 8192 | tf_op jit(solution)/shard_map/all_to_all | solution.py:57
  18.8 1.5 copy.42
  21.2 4.0 %all-to-all-done = s32[8,1,1]{2,1,0:T(1,128)S(1)} async-done(((s32[8,1,1]{2,1,0:T(1,128)}), s32[8,1,1]{2,1,0:T(1,128)S(1)}, u32[]{:S(2)}, u32[]{:S(2)}) %all-to-all-start) | async-done | bytes 64 | tf_op jit(solution)/shard_map/all_to_all | solution.py:57
  25.9 1.3 gather_fusion.1
  27.2 3.4 %all-to-all-start.1 = ((bf16[8,1,128,128]{3,2,1,0:T(8,128)(2,1)}), bf16[8,1,128,128]{3,2,1,0:T(8,128)(2,1)S(1)}, u32[]{:S(2)}, u32[]{:S(2)}) async-start(bf16[8,1,128,128]{3,2,1,0:T(8,128)(2,1)} %bitcast.22), calls=%async_computation.1 | async-start | bytes 524288 | tf_op jit(solution)/shard_map/all_to_all | solution.py:59
  30.8 8.0 %all-to-all-done.1 = bf16[8,1,128,128]{3,2,1,0:T(8,128)(2,1)S(1)} async-done(((bf16[8,1,128,128]{3,2,1,0:T(8,128)(2,1)}), bf16[8,1,128,128]{3,2,1,0:T(8,128)(2,1)S(1)}, u32[]{:S(2)}, u32[]{:S(2)}) %all-to-all-start.1) | async-done | bytes 262176 | tf_op jit(solution)/shard_map/all_to_all | solution.py:59
  39.6 8.3 %while.24 = (s32[]{:T(128)}, f32[2,128,2048]{2,1,0:T(8,128)}, bf16[2,128,16,128]{3,1,2,0:T(8,128)(2,1)S(1)}, bf16[2,16,128,128]{3,2,1,0:T(8,128)(2,1)S(1)}, f32[2,128,16]{1,2,0:T(8,128)S(1)}, /*index=5*/s32[]{:T(128)}) while((s32[]{:T(128)}, f32[2,128,2048]{2,1,0:T(8,128)}, bf16[2,128,16,128]{3,1,2,0:T(8,128)(2,1)S(1)}, ...), condition=%wide.region_6.7_spmd, body=%wide.region_4.6_spmd.sunk | while | flops 1086324736 | bytes 22044820 | solution.py:86
  39.7 2.6 %multiply_reduce_fusion.4 = f32[128,2048]{1,0:T(8,128)S(1)} fusion(f32[128,16]{0,1:T(8,128)S(1)} %dynamic-slice_bitcast_fusion.5, bf16[2048,128,1]{1,0,2:T(8,128)(2,1)S(1)} %bitcast.151, bf16[2,128,16,128]{3,1,2,0:T(8,128)(2,1)S(1)} %get-tuple-element.283, s32[]{:T(128)S(6)} %copy.90), kind=kOutput, calls=%fused_computation.6.clone.1 | convolution fusion | flops 1086062592 | bytes 2105348 | tf_op jit(solution)/shard_map/while/body/eval_jaxpr/qhd,kd->qhk/dot_general | solution.py:74
  42.4 1.3 copy-done.6
  43.8 2.6 %multiply_reduce_fusion.4 = f32[128,2048]{1,0:T(8,128)S(1)} fusion(f32[128,16]{0,1:T(8,128)S(1)} %dynamic-slice_bitcast_fusion.5, bf16[2048,128,1]{1,0,2:T(8,128)(2,1)S(1)} %bitcast.151, bf16[2,128,16,128]{3,1,2,0:T(8,128)(2,1)S(1)} %get-tuple-element.283, s32[]{:T(128)S(6)} %copy.90), kind=kOutput, calls=%fused_computation.6.clone.1 | convolution fusion | flops 1086062592 | bytes 2105348 | tf_op jit(solution)/shard_map/while/body/eval_jaxpr/qhd,kd->qhk/dot_general | solution.py:74
  46.6 1.3 copy-done.6
  51.8 46.2 %all-reduce.4.cloned.1.call-done = f32[256,2048]{1,0:T(8,128)} async-done(((f32[256,2048]{1,0:T(8,128)}), f32[256,2048]{1,0:T(8,128)}) %all-reduce.4.cloned.1.call-update) | async-done | bytes 2097168 | tf_op jit(solution)/shard_map/psum | solution.py:89
  98.0 2.9 %select_reduce_fusion.1 = (f32[256]{0:T(256)S(1)}, f32[256]{0:T(256)S(1)}) fusion(f32[256,2048]{1,0:T(8,128)} %all-reduce.4.cloned.1.call-done, pred[32,8,16,128]{3,2,1,0:T(8,128)(4,1)} %bitcast.152, bf16[256,2048]{1,0:T(8,128)(2,1)} %param.13), kind=kLoop, calls=%fused_computation.55 | loop fusion | flops 2620928 | bytes 3672064 | tf_op jit(solution)/shard_map/reduce_max | solution.py:14
  100.9 3.6 %select_reduce_fusion = (f32[]{:T(128)}, f32[256]{0:T(256)S(1)}) fusion(f32[256,2048]{1,0:T(8,128)S(1)} %copy-done, bf16[256,2048]{1,0:T(8,128)(2,1)} %param.13, f32[256]{0:T(256)S(1)} %get-tuple-element.134, pred[32,8,16,128]{3,2,1,0:T(8,128)(4,1)S(1)} %bitcast.154, f32[256]{0:T(256)S(1)} %get-tuple-element.133), kind=kLoop, calls=%fused_computation.48 | loop fusion | flops 6815487 | bytes 3673092 | tf_op jit(solution)/shard_map/reduce_sum | solution.py:92
  107.1 39.5 %all-reduce = (f32[]{:T(128)}, f32[]{:T(128)}) all-reduce(f32[]{:T(128)S(6)} %mul.105, f32[]{:T(128)S(6)} %mul.107), channel_id=1, replica_groups=mesh['seq'=8,'head'=4] {'seq','head'}, use_global_device_ids=true, to_apply=%region_12.13 | all-reduce | flops 2 | bytes 16 | tf_op jit(solution)/shard_map/psum | solution.py:101
  146.6 4.7 %multiply_divide_fusion = f32[256,2048]{1,0:T(8,128)} fusion(f32[256,2048]{1,0:T(8,128)S(1)} %copy-done, bf16[256,2048]{1,0:T(8,128)(2,1)} %param.13, f32[]{:T(128)} %get-tuple-element.163, f32[256]{0:T(256)S(1)} %get-tuple-element.134, f32[256]{0:T(256)S(1)} %get-tuple-element.132, f32[256]{0:T(256)S(1)} %get-tuple-element.133, ...), kind=kLoop, calls=%fused_computation.50 | loop fusion | flops 5767168 | bytes 5770244 | tf_op jit(solution)/shard_map/div | solution.py:106
  151.4 51.8 %while.25 = (s32[]{:T(128)}, bf16[2,128,16,128]{3,2,1,0:T(8,128)(2,1)}, f32[2,128,16]{1,0,2:T(2,128)S(1)}, f32[2,16,128,128]{3,2,1,0:T(8,128)}, bf16[2,128,16,12...) while((s32[]{:T(128)}, ...), condition=%wide.region_15.16_spmd, body=%wide.region_13.15_spmd.sunk | while | flops 3313502208 | bytes 61949172 | solution.py:130
  151.4 1.6 dynamic-slice_bitcast_fusion.6
  153.1 7.1 %fusion.74 = (u16[128,2048]{1,0:T(8,128)(2,1)S(1)}, f32[128,16,2048]{2,0,1:T(8,128)}) fusion(bf16[2048,128,1]{1,0,2:T(8,128)(2,1)S(1)} %bitcast.147, bf16[2,128,16,128]{3,1,2,0:T(8,128)(2,1)S(1)} %copy-done.3, s32[]{:T(128)S(6)} %copy.99), kind=kOutput, calls=%fused_computation.21.clone.1 | convolution fusion | flops 1094451200 | bytes 18350084 | tf_op jit(solution)/shard_map/while/body/eval_jaxpr/qhd,kd->qhk/dot_general | solution.py:74
  160.2 2.7 %fusion.75 = bf16[1,128,16,128]{3,1,2,0:T(8,128)(2,1)S(1)} fusion(bf16[2048,128,1]{1,0,2:T(8,128)(2,1)S(1)} %bitcast.148, f32[128,2048]{1,0:T(8,128)S(1)} %get-tuple-element.263, f32[128,16]{0,1:T(8,128)S(1)} %get-tuple-element.264, u16[128,2048]{1,0:T(8,128)(2,1)S(1)} %get-tuple-element.265), kind=kOutput, calls=%fused_computation.30.clone.1 | convolution fusion | flops 1103364096 | bytes 2629632 | tf_op jit(solution)/shard_map/while/body/eval_jaxpr/qhk,kd->qhd/dot_general | solution.py:122
  164.3 7.5 %multiply_reduce_fusion.5 = f32[128,16]{0,1:T(8,128)S(1)} fusion(f32[128,16,2048]{2,0,1:T(8,128)} %get-tuple-element.266, f32[128,2048]{1,0:T(8,128)S(1)} %get-tuple-element.263), kind=kLoop, calls=%fused_computation.19.clone.1 | loop fusion | flops 12580864 | bytes 17833984 | tf_op jit(solution)/shard_map/while/body/eval_jaxpr/reduce_sum | solution.py:113
  171.8 5.4 %fusion.76 = f32[2,16,128,128]{3,2,1,0:T(8,128)} fusion(f32[2,16,128,128]{3,2,1,0:T(8,128)} %get-tuple-element.300, s32[]{:T(128)S(6)} %copy.99, bf16[2,128,16,128]{3,1,2,0:T(8,128)(2,1)} %get-tuple-element.311, f32[2048,128]{0,1:T(8,128)S(1)} %get-tuple-element.267, f32[16,128]{1,0:T(8,128)S(1)} %get-tuple-element.268, u16[128,2048]{1,0:T(8,128)(2,1)} %copy-done.1), kind=kOutput, calls=%fused_computation.28.clone.1 | convolution fusion | flops 1103101952 | bytes 3154944 | tf_op jit(solution)/shard_map/while/body/eval_jaxpr/qhk,qhd->kd/dot_general | solution.py:125
  177.3 1.6 dynamic-slice_bitcast_fusion.6
  178.9 7.1 %fusion.74 = (u16[128,2048]{1,0:T(8,128)(2,1)S(1)}, f32[128,16,2048]{2,0,1:T(8,128)}) fusion(bf16[2048,128,1]{1,0,2:T(8,128)(2,1)S(1)} %bitcast.147, bf16[2,128,16,128]{3,1,2,0:T(8,128)(2,1)S(1)} %copy-done.3, s32[]{:T(128)S(6)} %copy.99), kind=kOutput, calls=%fused_computation.21.clone.1 | convolution fusion | flops 1094451200 | bytes 18350084 | tf_op jit(solution)/shard_map/while/body/eval_jaxpr/qhd,kd->qhk/dot_general | solution.py:74
  186.1 2.7 %fusion.75 = bf16[1,128,16,128]{3,1,2,0:T(8,128)(2,1)S(1)} fusion(bf16[2048,128,1]{1,0,2:T(8,128)(2,1)S(1)} %bitcast.148, f32[128,2048]{1,0:T(8,128)S(1)} %get-tuple-element.263, f32[128,16]{0,1:T(8,128)S(1)} %get-tuple-element.264, u16[128,2048]{1,0:T(8,128)(2,1)S(1)} %get-tuple-element.265), kind=kOutput, calls=%fused_computation.30.clone.1 | convolution fusion | flops 1103364096 | bytes 2629632 | tf_op jit(solution)/shard_map/while/body/eval_jaxpr/qhk,kd->qhd/dot_general | solution.py:122
  190.2 7.5 %multiply_reduce_fusion.5 = f32[128,16]{0,1:T(8,128)S(1)} fusion(f32[128,16,2048]{2,0,1:T(8,128)} %get-tuple-element.266, f32[128,2048]{1,0:T(8,128)S(1)} %get-tuple-element.263), kind=kLoop, calls=%fused_computation.19.clone.1 | loop fusion | flops 12580864 | bytes 17833984 | tf_op jit(solution)/shard_map/while/body/eval_jaxpr/reduce_sum | solution.py:113
  197.7 5.4 %fusion.76 = f32[2,16,128,128]{3,2,1,0:T(8,128)} fusion(f32[2,16,128,128]{3,2,1,0:T(8,128)} %get-tuple-element.300, s32[]{:T(128)S(6)} %copy.99, bf16[2,128,16,128]{3,1,2,0:T(8,128)(2,1)} %get-tuple-element.311, f32[2048,128]{0,1:T(8,128)S(1)} %get-tuple-element.267, f32[16,128]{1,0:T(8,128)S(1)} %get-tuple-element.268, u16[128,2048]{1,0:T(8,128)(2,1)} %copy-done.1), kind=kOutput, calls=%fused_computation.28.clone.1 | convolution fusion | flops 1103101952 | bytes 3154944 | tf_op jit(solution)/shard_map/while/body/eval_jaxpr/qhk,qhd->kd/dot_general | solution.py:125
  203.2 4.7 %scatter_fusion = f32[10,128,128]{2,1,0:T(8,128)S(1)} fusion(f32[10,128,128]{2,1,0:T(8,128)S(1)} %broadcast_in_dim.106, s32[32]{0:T(128)S(1)} %copy-done.11, f32[32,128,128]{2,1,0:T(8,128)} %bitcast.155), kind=kCustom, calls=%fused_computation.4 | custom fusion | flops 524288 | bytes 6291584 | tf_op jit(solution)/shard_map/scatter-add | solution.py:134
  208.6 5.3 %all-to-all-start.2 = ((bf16[8,1,128,128]{3,2,1,0:T(8,128)(2,1)}), bf16[8,1,128,128]{3,2,1,0:T(8,128)(2,1)S(1)}, u32[]{:S(2)}, u32[]{:S(2)}) async-start(bf16[8,1,128,128]{3,2,1,0:T(8,128)(2,1)} %fusion.39), calls=%async_computation.2 | async-start | bytes 524288 | tf_op jit(solution)/shard_map/all_to_all | solution.py:137
  213.9 8.4 %all-to-all-done.2 = bf16[8,1,128,128]{3,2,1,0:T(8,128)(2,1)S(1)} async-done(((bf16[8,1,128,128]{3,2,1,0:T(8,128)(2,1)}), bf16[8,1,128,128]{3,2,1,0:T(8,128)(2,1)S(1)}, u32[]{:S(2)}, u32[]{:S(2)}) %all-to-all-start.2) | async-done | bytes 262176 | tf_op jit(solution)/shard_map/all_to_all | solution.py:137
  226.0 28.0 %all-reduce.6.cloned.1.call-done = bf16[256,128]{1,0:T(8,128)(2,1)} async-done(((bf16[256,128]{1,0:T(8,128)(2,1)}), bf16[256,128]{1,0:T(8,128)(2,1)}) %all-reduce.6.cloned.1.call-update) | async-done | bytes 65552 | tf_op jit(solution)/shard_map/psum | solution.py:149
  254.1 1.5 reshape.246
  (105 shorter events, 17.8 us)
Async XLA Ops:
  8.7 17.2 %copy-start.7 = (bf16[256,128]{1,0:T(8,128)(2,1)S(1)}, bf16[256,128]{1,0:T(8,128)(2,1)}, u32[]{:S(2)}) copy-start(bf16[256,128]{1,0:T(8,128)(2,1)} %param.12) | copy-start | bytes 196612
  11.5 13.7 %all-to-all-start = ((s32[8,1,1]{2,1,0:T(1,128)}), s32[8,1,1]{2,1,0:T(1,128)S(1)}, u32[]{:S(2)}, u32[]{:S(2)}) async-start(s32[8,1,1]{2,1,0:T(1,128)} %copy.39), calls=%async_computation | async-start | bytes 8192 | tf_op jit(solution)/shard_map/all_to_all | solution.py:57
  18.8 12.0 %copy-start.9 = (bf16[256,16]{0,1:T(8,128)(2,1)S(1)}, bf16[256,16]{0,1:T(8,128)(2,1)}, u32[]{:S(2)}) copy-start(bf16[256,16]{0,1:T(8,128)(2,1)} %param.11) | copy-start | bytes 24580
  27.2 11.6 %all-to-all-start.1 = ((bf16[8,1,128,128]{3,2,1,0:T(8,128)(2,1)}), bf16[8,1,128,128]{3,2,1,0:T(8,128)(2,1)S(1)}, u32[]{:S(2)}, u32[]{:S(2)}) async-start(bf16[8,1,128,128]{3,2,1,0:T(8,128)(2,1)} %bitcast.22), calls=%async_computation.1 | async-start | bytes 524288 | tf_op jit(solution)/shard_map/all_to_all | solution.py:59
  30.6 67.3 %all-reduce.4.cloned.1.call-start = ((), (), s32[]{:S(2)}) async-start(), calls=%async_computation.3 | async-start | bytes 4194304 | tf_op jit(solution)/shard_map/psum | solution.py:89
  39.6 2.7 %copy-start.5 = (f32[2,128,2048]{2,1,0:T(8,128)S(1)}, f32[2,128,2048]{2,1,0:T(8,128)}, u32[]{:S(2)}) copy-start(f32[2,128,2048]{2,1,0:T(8,128)} %get-tuple-element.276) | copy-start | bytes 6291460 | tf_op jit(solution)/shard_map/while
  42.4 1.3 copy-start.6
  43.8 2.7 %copy-start.5 = (f32[2,128,2048]{2,1,0:T(8,128)S(1)}, f32[2,128,2048]{2,1,0:T(8,128)}, u32[]{:S(2)}) copy-start(f32[2,128,2048]{2,1,0:T(8,128)} %get-tuple-element.276) | copy-start | bytes 6291460 | tf_op jit(solution)/shard_map/while
  46.6 1.3 copy-start.6
  47.9 3.9 %copy-start.2 = (bf16[2,128,16,128]{3,1,2,0:T(8,128)(2,1)}, bf16[2,128,16,128]{3,1,2,0:T(8,128)(2,1)S(1)}, u32[]{:S(2)}) copy-start(bf16[2,128,16,128]{3,1,2,0:T(8,128)(2,1)S(1)} %get-tuple-element.321) | copy-start | bytes 3145732
  47.9 0.7 copy-start.14
  47.9 0.7 copy-start.8
  98.0 2.9 %copy-start = (f32[256,2048]{1,0:T(8,128)S(1)}, f32[256,2048]{1,0:T(8,128)}, u32[]{:S(2)}) copy-start(f32[256,2048]{1,0:T(8,128)} %all-reduce.4.cloned.1.call-done) | copy-start | bytes 6291460
  98.0 2.9 %copy-start.4 = (pred[2,128,16,128]{3,2,1,0:T(8,128)(4,1)S(1)}, pred[2,128,16,128]{3,2,1,0:T(8,128)(4,1)}, u32[]{:S(2)}) copy-start(pred[2,128,16,128]{3,2,1,0:T(8,128)(4,1)} %or_and_fusion) | copy-start | bytes 1572868
  151.4 51.8 %copy-start.11 = (s32[32]{0:T(128)S(1)}, s32[32]{0:T(128)}, u32[]{:S(2)}) copy-start(s32[32]{0:T(128)} %reshape.283) | copy-start | bytes 388
  151.4 1.7 copy-start.3
  160.2 2.7 %copy-start.1 = (u16[128,2048]{1,0:T(8,128)(2,1)}, u16[128,2048]{1,0:T(8,128)(2,1)S(1)}, u32[]{:S(2)}) copy-start(u16[128,2048]{1,0:T(8,128)(2,1)S(1)} %get-tuple-element.265) | copy-start | bytes 1572868 | tf_op jit(solution)/shard_map/while
  160.2 2.7 %copy-start.12 = (bf16[2,128,16,128]{3,2,1,0:T(8,128)(2,1)S(1)}, bf16[2,128,16,128]{3,2,1,0:T(8,128)(2,1)}, u32[]{:S(2)}) copy-start(bf16[2,128,16,128]{3,2,1,0:T(8,128)(2,1)} %get-tuple-element.298) | copy-start | bytes 3145732 | tf_op jit(solution)/shard_map/while
  163.3 1.0 copy-start.13
  177.3 1.7 copy-start.3
  186.1 2.7 %copy-start.1 = (u16[128,2048]{1,0:T(8,128)(2,1)}, u16[128,2048]{1,0:T(8,128)(2,1)S(1)}, u32[]{:S(2)}) copy-start(u16[128,2048]{1,0:T(8,128)(2,1)S(1)} %get-tuple-element.265) | copy-start | bytes 1572868 | tf_op jit(solution)/shard_map/while
  186.1 2.7 %copy-start.12 = (bf16[2,128,16,128]{3,2,1,0:T(8,128)(2,1)S(1)}, bf16[2,128,16,128]{3,2,1,0:T(8,128)(2,1)}, u32[]{:S(2)}) copy-start(bf16[2,128,16,128]{3,2,1,0:T(8,128)(2,1)} %get-tuple-element.298) | copy-start | bytes 3145732 | tf_op jit(solution)/shard_map/while
  189.2 1.0 copy-start.13
  207.9 14.6 %copy-start.10 = (s32[8]{0:T(128)S(1)}, s32[8]{0:T(128)}, u32[]{:S(2)}) copy-start(s32[8]{0:T(128)} %get-tuple-element.135) | copy-start | bytes 100
  208.6 13.8 %all-to-all-start.2 = ((bf16[8,1,128,128]{3,2,1,0:T(8,128)(2,1)}), bf16[8,1,128,128]{3,2,1,0:T(8,128)(2,1)S(1)}, u32[]{:S(2)}, u32[]{:S(2)}) async-start(bf16[8,1,128,128]{3,2,1,0:T(8,128)(2,1)} %fusion.39), calls=%async_computation.2 | async-start | bytes 524288 | tf_op jit(solution)/shard_map/all_to_all | solution.py:137
  213.9 40.2 %all-reduce.6.cloned.1.call-start = ((), (), s32[]{:S(2)}) async-start(), calls=%async_computation.4 | async-start | bytes 131072 | tf_op jit(solution)/shard_map/psum | solution.py:149
Sparse Core Ops, SparseCore 0:
  48.0 49.9 all-reduce.3
  224.3 29.7 all-reduce.5
where the time goes:
time: 265 us; the launch traced here: 264 us
  waiting for transfers between devices  94.7 us (36%)
  other arithmetic  40.9 us (15%)
  blocking collectives  39.5 us (15%)
  matrix products  35.8 us (14%)
  between operations  18.6 us (7%)
  local copies, waits for them, and re-layouts  17.7 us (7%)
  starting transfers between devices  16 us (6%)
    psum x1, waiting for transfers between devices, local(): score_part = lax.psum(partial_value, 'head')  46.2 us
    psum x1, blocking collectives, local(): lax.psum((loss_part, is_first * pair_local), ('seq', 'head'))  39.5 us
    psum x1, waiting for transfers between devices, local(): lax.psum(owned_grad.astype(jnp.bfloat16), 'head').astype(jnp.float32)  28 us
    dot_general x4, matrix products, dot_values(): jnp.einsum('qhd,kd->qhk', query_tile, key_tile.reshape(-1, key_width), pr...  19.5 us
    reduce_sum x2, other arithmetic, backward(): jnp.sum(jnp.maximum(values, 0.0) * grad_tile[:, None, :], axis=2)  14.9 us
    dot_general x2, matrix products, backward(): jnp.einsum('qhk,qhd->kd', dot_grads, query_tile, preferred_element_type=j...  10.9 us
    all_to_all x1, waiting for transfers between devices, local(): lax.all_to_all(spread[tiles_here:].reshape(owner_count, CAP, BLOCK, key_w...  8.45 us
    all_to_all x1, waiting for transfers between devices, local(): lax.all_to_all(reply_blocks, 'seq', split_axis=0, concat_axis=0, tiled=True)  7.99 us
  transfers between devices with their start and end apart: 5, of which 5 were waited for; matrix products, arithmetic and copies ran while one was open for 2% of the time, Pallas kernels for 0%

commit v1 on v0

--- a/solution.py
+++ b/solution.py
@@ -86,7 +86,7 @@
     partial_value = lax.map(forward, (query_tiles, weight_tiles, fetched)).reshape(row_count, KEYS)
     target_vals = jnp.where(live_mask, targets.astype(jnp.float32), 0.0)
     pair_local = jnp.sum(live_mask.astype(jnp.float32))
-    score_part = lax.psum(partial_value, "head")
+    score_part = jnp.sum(lax.all_gather(partial_value, "head"), axis=0)
     row_max, row_norm, row_target = row_statistics(score_part, live_mask, target_vals)
     target_prob = jnp.where(live_mask, target_vals / row_target[:, None], 0.0)
     kl_cols = jnp.sum(

time: 265 us -> 274 us (1.034)
  waiting for transfers between devices: 94.7 us -> 102 us
    all_gather x0 -> x1, waiting for transfers between devices: none -> 53.1 us  [local(): score_part = jnp.sum(lax.all_gather(partial_value, 'head'), axis=0)]
    psum x1 -> x0, waiting for transfers between devices: 46.2 us -> none  [local(): score_part = lax.psum(partial_value, 'head')]
    reduce_sum x0 -> x1, other arithmetic: none -> 4.4 us  [local(): score_part = jnp.sum(lax.all_gather(partial_value, 'head'), axis=0)]
where the time goes in v1:
time: 274 us; the launch traced here: 273 us
  waiting for transfers between devices  102 us (37%)
  other arithmetic  43.4 us (16%)
  blocking collectives  39.4 us (14%)
  matrix products  35.8 us (13%)
  between operations  18.5 us (7%)
  local copies, waits for them, and re-layouts  17.9 us (7%)
  starting transfers between devices  16 us (6%)
    all_gather x1, waiting for transfers between devices, local(): score_part = jnp.sum(lax.all_gather(partial_value, 'head'), axis=0)  53.1 us
    psum x1, blocking collectives, local(): lax.psum((loss_part, is_first * pair_local), ('seq', 'head'))  39.4 us
    psum x1, waiting for transfers between devices, local(): lax.psum(owned_grad.astype(jnp.bfloat16), 'head').astype(jnp.float32)  28.1 us
    dot_general x4, matrix products, dot_values(): jnp.einsum('qhd,kd->qhk', query_tile, key_tile.reshape(-1, key_width), pr...  19.5 us
    reduce_sum x2, other arithmetic, backward(): jnp.sum(jnp.maximum(values, 0.0) * grad_tile[:, None, :], axis=2)  14.9 us
    dot_general x2, matrix products, backward(): jnp.einsum('qhk,qhd->kd', dot_grads, query_tile, preferred_element_type=j...  10.9 us
    all_to_all x1, waiting for transfers between devices, local(): lax.all_to_all(spread[tiles_here:].reshape(owner_count, CAP, BLOCK, key_w...  8.47 us
    all_to_all x1, waiting for transfers between devices, local(): lax.all_to_all(reply_blocks, 'seq', split_axis=0, concat_axis=0, tiled=True)  7.99 us
  transfers between devices with their start and end apart: 5, of which 5 were waited for; matrix products, arithmetic and copies ran while one was open for 2% of the time, Pallas kernels for 0%

profile of v1, /device:TPU:0, one launch (start us, length us, event | category | flops | bytes accessed | tf_op | source)
XLA Modules:
  0.0 273.0 jit_solution(12194441531059110639)
XLA Ops:
  11.5 7.3 %all-to-all-start = ((s32[8,1,1]{2,1,0:T(1,128)}), s32[8,1,1]{2,1,0:T(1,128)S(1)}, u32[]{:S(2)}, u32[]{:S(2)}) async-start(s32[8,1,1]{2,1,0:T(1,128)} %copy.39), calls=%async_computation | async-start | bytes 8192 | tf_op jit(solution)/shard_map/all_to_all | solution.py:57
  18.8 1.5 copy.42
  21.2 4.0 %all-to-all-done = s32[8,1,1]{2,1,0:T(1,128)S(1)} async-done(((s32[8,1,1]{2,1,0:T(1,128)}), s32[8,1,1]{2,1,0:T(1,128)S(1)}, u32[]{:S(2)}, u32[]{:S(2)}) %all-to-all-start) | async-done | bytes 64 | tf_op jit(solution)/shard_map/all_to_all | solution.py:57
  27.2 3.4 %all-to-all-start.1 = ((bf16[8,1,128,128]{3,2,1,0:T(8,128)(2,1)}), bf16[8,1,128,128]{3,2,1,0:T(8,128)(2,1)S(1)}, u32[]{:S(2)}, u32[]{:S(2)}) async-start(bf16[8,1,128,128]{3,2,1,0:T(8,128)(2,1)} %bitcast.22), calls=%async_computation.1 | async-start | bytes 524288 | tf_op jit(solution)/shard_map/all_to_all | solution.py:59
  30.8 8.0 %all-to-all-done.1 = bf16[8,1,128,128]{3,2,1,0:T(8,128)(2,1)S(1)} async-done(((bf16[8,1,128,128]{3,2,1,0:T(8,128)(2,1)}), bf16[8,1,128,128]{3,2,1,0:T(8,128)(2,1)S(1)}, u32[]{:S(2)}, u32[]{:S(2)}) %all-to-all-start.1) | async-done | bytes 262176 | tf_op jit(solution)/shard_map/all_to_all | solution.py:59
  39.6 8.5 %while.24 = (s32[]{:T(128)}, f32[2,128,2048]{2,1,0:T(8,128)}, bf16[2,128,16,128]{3,1,2,0:T(8,128)(2,1)S(1)}, bf16[2,16,128,128]{3,2,1,0:T(8,128)(2,1)S(1)}, f32[2,128,16]{1,2,0:T(8,128)S(1)}, /*index=5*/s32[]{:T(128)}) while((s32[]{:T(128)}, f32[2,128,2048]{2,1,0:T(8,128)}, bf16[2,128,16,128]{3,1,2,0:T(8,128)(2,1)S(1)}, ...), condition=%wide.region_6.7_spmd, body=%wide.region_4.6_spmd.sunk | while | flops 1086324736 | bytes 22044820 | solution.py:86
  39.7 2.6 multiply_reduce_fusion.4
  42.4 1.4 copy-done.6
  43.9 2.6 multiply_reduce_fusion.4
  46.7 1.4 copy-done.6
  52.0 53.1 %all-gather.2.cloned.1.call-done = f32[4,256,2048]{2,1,0:T(8,128)} async-done(((f32[1,256,2048]{2,1,0:T(8,128)}), f32[4,256,2048]{2,1,0:T(8,128)}) %all-gather.2.cloned.1.call-update) | async-done | bytes 8388624 | tf_op jit(solution)/shard_map/all_gather | solution.py:89
  105.1 4.4 %reduce_sum.92 = f32[256,2048]{1,0:T(8,128)S(1)} reduce(f32[4,256,2048]{2,1,0:T(8,128)} %all-gather.2.cloned.1.call-done, f32[]{:T(128)} %constant.68.clone.1), dimensions={0}, to_apply=%region_7.8 | reduce | flops 1572864 | bytes 10485764 | tf_op jit(solution)/shard_map/reduce_sum | solution.py:89
  109.5 2.2 select_reduce_fusion.1
  111.7 2.4 select_reduce_fusion
  116.5 39.4 %all-reduce = (f32[]{:T(128)}, f32[]{:T(128)}) all-reduce(f32[]{:T(128)S(6)} %mul.105, f32[]{:T(128)S(6)} %mul.107), channel_id=1, replica_groups=mesh['seq'=8,'head'=4] {'seq','head'}, use_global_device_ids=true, to_apply=%region_12.13 | all-reduce | flops 2 | bytes 16 | tf_op jit(solution)/shard_map/psum | solution.py:101
  156.0 4.7 %multiply_divide_fusion = f32[256,2048]{1,0:T(8,128)} fusion(f32[256,2048]{1,0:T(8,128)S(1)} %reduce_sum.92, bf16[256,2048]{1,0:T(8,128)(2,1)} %param.13, f32[]{:T(128)} %get-tuple-element.163, f32[256]{0:T(256)S(1)} %get-tuple-element.134, f32[256]{0:T(256)S(1)} %get-tuple-element.132, f32[256]{0:T(256)S(1)} %get-tuple-element.133, ...), kind=kLoop, calls=%fused_computation.50 | loop fusion | flops 5767168 | bytes 5770244 | tf_op jit(solution)/shard_map/div | solution.py:106
  160.7 51.8 %while.25 = (s32[]{:T(128)}, bf16[2,128,16,128]{3,2,1,0:T(8,128)(2,1)}, f32[2,128,16]{1,0,2:T(2,128)S(1)}, f32[2,16,128,128]{3,2,1,0:T(8,128)}, bf16[2,128,16,12...) while((s32[]{:T(128)}, ...), condition=%wide.region_15.16_spmd, body=%wide.region_13.15_spmd.sunk | while | flops 3313502208 | bytes 61949172 | solution.py:130
  160.8 1.6 dynamic-slice_bitcast_fusion.6
  162.4 7.1 %fusion.74 = (u16[128,2048]{1,0:T(8,128)(2,1)S(1)}, f32[128,16,2048]{2,0,1:T(8,128)}) fusion(bf16[2048,128,1]{1,0,2:T(8,128)(2,1)S(1)} %bitcast.147, bf16[2,128,16,128]{3,1,2,0:T(8,128)(2,1)S(1)} %copy-done.2, s32[]{:T(128)S(6)} %copy.99), kind=kOutput, calls=%fused_computation.21.clone.1 | convolution fusion | flops 1094451200 | bytes 18350084 | tf_op jit(solution)/shard_map/while/body/eval_jaxpr/qhd,kd->qhk/dot_general | solution.py:74
  169.5 2.7 fusion.75
  173.6 7.5 %multiply_reduce_fusion.5 = f32[128,16]{0,1:T(8,128)S(1)} fusion(f32[128,16,2048]{2,0,1:T(8,128)} %get-tuple-element.266, f32[128,2048]{1,0:T(8,128)S(1)} %get-tuple-element.263), kind=kLoop, calls=%fused_computation.19.clone.1 | loop fusion | flops 12580864 | bytes 17833984 | tf_op jit(solution)/shard_map/while/body/eval_jaxpr/reduce_sum | solution.py:113
  181.1 5.4 %fusion.76 = f32[2,16,128,128]{3,2,1,0:T(8,128)} fusion(f32[2,16,128,128]{3,2,1,0:T(8,128)} %get-tuple-element.300, s32[]{:T(128)S(6)} %copy.99, bf16[2,128,16,128]{3,1,2,0:T(8,128)(2,1)} %get-tuple-element.311, f32[2048,128]{0,1:T(8,128)S(1)} %get-tuple-element.267, f32[16,128]{1,0:T(8,128)S(1)} %get-tuple-element.268, u16[128,2048]{1,0:T(8,128)(2,1)} %copy-done), kind=kOutput, calls=%fused_computation.28.clone.1 | convolution fusion | flops 1103101952 | bytes 3154944 | tf_op jit(solution)/shard_map/while/body/eval_jaxpr/qhk,qhd->kd/dot_general | solution.py:125
  186.6 1.6 dynamic-slice_bitcast_fusion.6
  188.3 7.1 %fusion.74 = (u16[128,2048]{1,0:T(8,128)(2,1)S(1)}, f32[128,16,2048]{2,0,1:T(8,128)}) fusion(bf16[2048,128,1]{1,0,2:T(8,128)(2,1)S(1)} %bitcast.147, bf16[2,128,16,128]{3,1,2,0:T(8,128)(2,1)S(1)} %copy-done.2, s32[]{:T(128)S(6)} %copy.99), kind=kOutput, calls=%fused_computation.21.clone.1 | convolution fusion | flops 1094451200 | bytes 18350084 | tf_op jit(solution)/shard_map/while/body/eval_jaxpr/qhd,kd->qhk/dot_general | solution.py:74
  195.4 2.7 fusion.75
  199.5 7.5 %multiply_reduce_fusion.5 = f32[128,16]{0,1:T(8,128)S(1)} fusion(f32[128,16,2048]{2,0,1:T(8,128)} %get-tuple-element.266, f32[128,2048]{1,0:T(8,128)S(1)} %get-tuple-element.263), kind=kLoop, calls=%fused_computation.19.clone.1 | loop fusion | flops 12580864 | bytes 17833984 | tf_op jit(solution)/shard_map/while/body/eval_jaxpr/reduce_sum | solution.py:113
  207.0 5.4 %fusion.76 = f32[2,16,128,128]{3,2,1,0:T(8,128)} fusion(f32[2,16,128,128]{3,2,1,0:T(8,128)} %get-tuple-element.300, s32[]{:T(128)S(6)} %copy.99, bf16[2,128,16,128]{3,1,2,0:T(8,128)(2,1)} %get-tuple-element.311, f32[2048,128]{0,1:T(8,128)S(1)} %get-tuple-element.267, f32[16,128]{1,0:T(8,128)S(1)} %get-tuple-element.268, u16[128,2048]{1,0:T(8,128)(2,1)} %copy-done), kind=kOutput, calls=%fused_computation.28.clone.1 | convolution fusion | flops 1103101952 | bytes 3154944 | tf_op jit(solution)/shard_map/while/body/eval_jaxpr/qhk,qhd->kd/dot_general | solution.py:125
  212.5 4.7 %scatter_fusion = f32[10,128,128]{2,1,0:T(8,128)S(1)} fusion(f32[10,128,128]{2,1,0:T(8,128)S(1)} %broadcast_in_dim.106, s32[32]{0:T(128)S(1)} %copy-done.11, f32[32,128,128]{2,1,0:T(8,128)} %bitcast.155), kind=kCustom, calls=%fused_computation.4 | custom fusion | flops 524288 | bytes 6291584 | tf_op jit(solution)/shard_map/scatter-add | solution.py:134
  217.9 5.3 %all-to-all-start.2 = ((bf16[8,1,128,128]{3,2,1,0:T(8,128)(2,1)}), bf16[8,1,128,128]{3,2,1,0:T(8,128)(2,1)S(1)}, u32[]{:S(2)}, u32[]{:S(2)}) async-start(bf16[8,1,128,128]{3,2,1,0:T(8,128)(2,1)} %fusion.39), calls=%async_computation.2 | async-start | bytes 524288 | tf_op jit(solution)/shard_map/all_to_all | solution.py:137
  223.3 8.5 %all-to-all-done.2 = bf16[8,1,128,128]{3,2,1,0:T(8,128)(2,1)S(1)} async-done(((bf16[8,1,128,128]{3,2,1,0:T(8,128)(2,1)}), bf16[8,1,128,128]{3,2,1,0:T(8,128)(2,1)S(1)}, u32[]{:S(2)}, u32[]{:S(2)}) %all-to-all-start.2) | async-done | bytes 262176 | tf_op jit(solution)/shard_map/all_to_all | solution.py:137
  235.4 28.1 %all-reduce.3.cloned.1.call-done = bf16[256,128]{1,0:T(8,128)(2,1)} async-done(((bf16[256,128]{1,0:T(8,128)(2,1)}), bf16[256,128]{1,0:T(8,128)(2,1)}) %all-reduce.3.cloned.1.call-update) | async-done | bytes 65552 | tf_op jit(solution)/shard_map/psum | solution.py:149
  263.5 1.5 reshape.286
  (106 shorter events, 19.0 us)
Async XLA Ops:
  8.7 17.2 %copy-start.7 = (bf16[256,128]{1,0:T(8,128)(2,1)S(1)}, bf16[256,128]{1,0:T(8,128)(2,1)}, u32[]{:S(2)}) copy-start(bf16[256,128]{1,0:T(8,128)(2,1)} %param.12) | copy-start | bytes 196612
  11.5 13.7 %all-to-all-start = ((s32[8,1,1]{2,1,0:T(1,128)}), s32[8,1,1]{2,1,0:T(1,128)S(1)}, u32[]{:S(2)}, u32[]{:S(2)}) async-start(s32[8,1,1]{2,1,0:T(1,128)} %copy.39), calls=%async_computation | async-start | bytes 8192 | tf_op jit(solution)/shard_map/all_to_all | solution.py:57
  18.8 12.0 %copy-start.9 = (bf16[256,16]{0,1:T(8,128)(2,1)S(1)}, bf16[256,16]{0,1:T(8,128)(2,1)}, u32[]{:S(2)}) copy-start(bf16[256,16]{0,1:T(8,128)(2,1)} %param.11) | copy-start | bytes 24580
  27.2 11.6 %all-to-all-start.1 = ((bf16[8,1,128,128]{3,2,1,0:T(8,128)(2,1)}), bf16[8,1,128,128]{3,2,1,0:T(8,128)(2,1)S(1)}, u32[]{:S(2)}, u32[]{:S(2)}) async-start(bf16[8,1,128,128]{3,2,1,0:T(8,128)(2,1)} %bitcast.22), calls=%async_computation.1 | async-start | bytes 524288 | tf_op jit(solution)/shard_map/all_to_all | solution.py:59
  30.6 74.5 %all-gather.2.cloned.1.call-start = ((), (), s32[]{:S(2)}) async-start(), calls=%async_computation.3 | async-start | bytes 10485760 | tf_op jit(solution)/shard_map/all_gather | solution.py:89
  39.6 2.7 copy-start.5
  42.4 1.4 copy-start.6
  43.9 2.7 copy-start.5
  46.7 1.4 copy-start.6
  48.1 4.0 %copy-start.1 = (bf16[2,128,16,128]{3,1,2,0:T(8,128)(2,1)}, bf16[2,128,16,128]{3,1,2,0:T(8,128)(2,1)S(1)}, u32[]{:S(2)}) copy-start(bf16[2,128,16,128]{3,1,2,0:T(8,128)(2,1)S(1)} %get-tuple-element.320) | copy-start | bytes 3145732
  48.1 0.7 copy-start.14
  48.1 0.7 copy-start.8
  109.5 2.2 copy-start.3
  109.5 2.2 copy-start.4
  160.7 51.8 %copy-start.11 = (s32[32]{0:T(128)S(1)}, s32[32]{0:T(128)}, u32[]{:S(2)}) copy-start(s32[32]{0:T(128)} %reshape.323) | copy-start | bytes 388
  160.7 1.7 copy-start.2
  169.5 2.7 copy-start
  169.5 2.7 copy-start.12
  172.6 1.0 copy-start.13
  186.6 1.7 copy-start.2
  195.4 2.7 copy-start
  195.4 2.7 copy-start.12
  198.5 1.0 copy-start.13
  217.2 14.6 %copy-start.10 = (s32[8]{0:T(128)S(1)}, s32[8]{0:T(128)}, u32[]{:S(2)}) copy-start(s32[8]{0:T(128)} %get-tuple-element.135) | copy-start | bytes 100
  217.9 13.8 %all-to-all-start.2 = ((bf16[8,1,128,128]{3,2,1,0:T(8,128)(2,1)}), bf16[8,1,128,128]{3,2,1,0:T(8,128)(2,1)S(1)}, u32[]{:S(2)}, u32[]{:S(2)}) async-start(bf16[8,1,128,128]{3,2,1,0:T(8,128)(2,1)} %fusion.39), calls=%async_computation.2 | async-start | bytes 524288 | tf_op jit(solution)/shard_map/all_to_all | solution.py:137
  223.2 40.3 %all-reduce.3.cloned.1.call-start = ((), (), s32[]{:S(2)}) async-start(), calls=%async_computation.4 | async-start | bytes 131072 | tf_op jit(solution)/shard_map/psum | solution.py:149
Sparse Core Ops, SparseCore 0:
  48.2 56.8 all-gather.1
  233.6 29.8 all-reduce.2
